TPU v7x, 32 devices: a whole 2x2x4 slice. The times are simulated.
32 devices in a mesh: dp: 8 (over z, x), tp: 4 (over y, core).
Axes of the slice: x: 2, y: 2, z: 4, core: 2. Of those that a mesh axis runs over, the one named last changes fastest.
Arguments:
- slopes: bfloat16 [8, 2, 3072, 768], P('dp', None, 'tp'), may hold values from -6 to 6, as said below
- basis_in: float32 [2, 768, 8], replicated, may hold values from -6 to 6
- weights_in: float32 [2, 3072, 768], P(None, 'tp', 'dp'), may hold values from -0.21875 to 0.21875
Outputs:
- new_weights: float32 [2, 3072, 768], P(None, 'tp', 'dp')
- new_basis: float32 [2, 768, 8], replicated
Inputs may be any that keep to these rules, and one draw needn't show every extreme that they name: slopes holds numbers from -6 to 6.
All inputs are finite; a program needn't handle non-finite values.
Results may differ from a plain program's by a relative error of at most 0.0003.
Values sent between devices are 32-bit elements.
A program may use at most 64 MiB of HBM per device.

v0:
```python
import jax
import jax.numpy as jnp
from jax import lax
from jax.sharding import PartitionSpec as P

RANK = 8


def body(slopes, basis_in, weights_in):
    own_grads = slopes[0]
    part_left = jnp.einsum(
        "liw,lwr->lir", own_grads, basis_in.astype(jnp.bfloat16), preferred_element_type=jnp.float32
    )
    left = lax.psum(part_left, "dp")
    part_gram = jnp.einsum("lir,lis->lrs", left, left, precision=lax.Precision.HIGHEST)
    small_left = left.astype(jnp.bfloat16)
    part_right = jnp.einsum(
        "liw,lir->lwr", own_grads, small_left, preferred_element_type=jnp.float32
    )
    own_share = part_gram / lax.axis_size("dp")
    right, gram = lax.psum((part_right, own_share), ("dp", "tp"))
    gram = gram + 0.001 * jnp.mean(jnp.diagonal(gram, axis1=1, axis2=2), axis=1)[
        :, None, None
    ] * jnp.eye(RANK, dtype=jnp.float32)
    place = lax.axis_index("dp") * weights_in.shape[2]
    own_right = lax.dynamic_slice_in_dim(right, place, weights_in.shape[2], axis=1)
    root = jnp.linalg.cholesky(gram)
    half = lax.linalg.triangular_solve(
        root, jnp.swapaxes(own_right, 1, 2), left_side=True, lower=True
    )
    mixed = lax.linalg.triangular_solve(root, half, left_side=True, lower=True, transpose_a=True)
    change = jnp.einsum(
        "lir,lrw->liw", left, mixed, precision=lax.Precision.HIGHEST
    ) / lax.axis_size("dp")
    new_weights = weights_in - 0.02 * change
    new_basis = right * lax.rsqrt(jnp.mean(right * right, axis=(1, 2), keepdims=True) + 1e-12)
    return (new_weights, new_basis)


def solution(mesh):
    placed = (P("dp", None, "tp", None), P(), P(None, "tp", "dp"))
    return jax.shard_map(
        body, mesh=mesh, in_specs=placed, out_specs=(P(None, "tp", "dp"), P()), check_vma=False
    )
```

profile of v0, /device:TPU:14, one launch (start us, length us, event | category | flops | bytes accessed | tf_op | source)
XLA Modules:
  0.0 88.3 jit_solution(12999612383202632761)
XLA Ops:
  0.6 0.0 copy-start
  0.7 0.1 copy.11
  0.8 1.5 %copy-done = bf16[1,2,768,768]{3,2,1,0:T(8,128)(2,1)S(1)} copy-done((bf16[1,2,768,768]{3,2,1,0:T(8,128)(2,1)S(1)}, bf16[1,2,768,768]{3,2,1,0:T(8,128)(2,1)}, u32[]{:S(2)}) %copy-start) | copy-done | bytes 2359320
  2.3 1.6 %fusion.2 = f32[2,768,8]{1,2,0:T(8,128)S(1)} fusion(bf16[1,2,768,768]{3,2,1,0:T(8,128)(2,1)S(1)} %copy-done, f32[2,768,8]{1,2,0:T(8,128)} %param.4), kind=kOutput, calls=%fused_computation.3 | convolution fusion | flops 18886656 | bytes 2457600 | tf_op jit(solution)/shard_map/liw,lwr->lir/dot_general | solution.py:11
  3.9 30.6 %psum.21 = f32[2,768,8]{1,2,0:T(8,128)S(1)} all-reduce(f32[2,768,8]{1,2,0:T(8,128)S(1)} %fusion.2), channel_id=1, replica_groups=mesh['dp'=8,'tp'=4] {'dp'}, use_global_device_ids=true, to_apply=%region_0.0 | all-reduce | flops 12288 | bytes 98304 | tf_op jit(solution)/shard_map/psum | solution.py:14
  34.4 0.2 convolution_multiply_fusion.1
  34.6 0.4 fusion.5
  35.0 46.7 %all-reduce = (f32[2,8,8]{1,2,0:T(8,128)S(1)}, f32[2,768,8]{1,2,0:T(8,128)S(1)}) all-reduce(f32[2,8,8]{1,2,0:T(8,128)S(1)} %convolution_multiply_fusion.1, f32[2,768,8]{1,2,0:T(8,128)S(1)} %fusion.5), channel_id=1, replica_groups=mesh['dp'=8,'tp'=4] {'dp','tp'}, use_global_device_ids=true, to_apply=%region_1.0 | all-reduce | flops 12416 | bytes 99328 | tf_op jit(solution)/shard_map/psum | solution.py:21
  81.7 0.1 multiply_reduce_fusion
  81.8 0.1 copy.13
  82.0 0.6 gather_fusion
  82.6 0.1 multiply_add_fusion
  82.6 0.1 copy.14
  82.7 0.1 fusion.14
  82.8 1.4 %custom-call.9 = f32[2,8,8]{2,1,0:T(8,128)S(1)} custom-call(f32[2,8,8]{2,1,0:T(8,128)S(1)} %fusion.14), custom_call_target="Cholesky" | custom-call | tf_op jit(solution)/shard_map/jit(cholesky)/cholesky | solution.py:27
  84.2 0.1 select_reduce_fusion
  84.3 0.1 compare_reduce_fusion
  84.4 0.1 select_bitcast_fusion
  84.5 1.3 %custom-call.10 = f32[2,1,8,8]{2,3,1,0:T(8,128)S(1)} custom-call(f32[2,1,8,8]{3,2,1,0:T(8,128)S(1)} %select_bitcast_fusion), custom_call_target="InvertDiagBlocksLowerTriangular" | custom-call | tf_op jit(solution)/shard_map/triangular_solve | solution.py:31
  85.7 0.2 fusion.10
  86.0 0.1 fusion.12
  86.1 0.7 broadcast_multiply_fusion
  86.8 0.0 copy-done.1
  86.8 1.5 %fusion.4 = f32[2,768,96]{1,2,0:T(8,128)} fusion(f32[2,768,96]{1,2,0:T(8,128)S(1)} %copy-done.1, f32[2,768,8]{1,2,0:T(8,128)S(1)} %psum.21, f32[2,8,96]{2,1,0:T(8,128)S(1)} %fusion.12), kind=kOutput, calls=%fused_computation.6 | convolution fusion | flops 14450688 | bytes 1234944 | tf_op jit(solution)/shard_map/lir,lrw->liw/dot_general | solution.py:32
  (8 shorter events, 0.1 us)
Async XLA Ops:
  0.6 1.7 %copy-start = (bf16[1,2,768,768]{3,2,1,0:T(8,128)(2,1)S(1)}, bf16[1,2,768,768]{3,2,1,0:T(8,128)(2,1)}, u32[]{:S(2)}) copy-start(bf16[1,2,768,768]{3,2,1,0:T(8,128)(2,1)} %param.3) | copy-start | bytes 7077892
  2.3 84.5 %copy-start.1 = (f32[2,768,96]{1,2,0:T(8,128)S(1)}, f32[2,768,96]{1,2,0:T(8,128)}, u32[]{:S(2)}) copy-start(f32[2,768,96]{1,2,0:T(8,128)} %param.5) | copy-start | bytes 1769476
where the time goes:
time: 88.6 us; the launch traced here: 88.3 us
  blocking collectives  77.2 us (87%)
  matrix products  4.02 us (5%)
  other arithmetic  3.96 us (4%)
  local copies, waits for them, and re-layouts  2.39 us (3%)
    psum x1, blocking collectives, body(): right, gram = lax.psum((part_right, own_share), ('dp', 'tp'))  46.7 us
    psum x1, blocking collectives, body(): left = lax.psum(part_left, 'dp')  30.6 us

commit v1 on v0

--- a/solution.py
+++ b/solution.py
@@ -11,7 +11,7 @@
     part_left = jnp.einsum(
         "liw,lwr->lir", own_grads, basis_in.astype(jnp.bfloat16), preferred_element_type=jnp.float32
     )
-    left = lax.psum(part_left, "dp")
+    left = jnp.sum(lax.all_gather(part_left, "dp"), axis=0)
     part_gram = jnp.einsum("lir,lis->lrs", left, left, precision=lax.Precision.HIGHEST)
     small_left = left.astype(jnp.bfloat16)
     part_right = jnp.einsum(

time: 88.6 us -> 84.4 us (0.953); the launches traced: 88.3 us -> 83 us
  blocking collectives: 77.2 us -> 71.9 us
    psum x1 -> x0, blocking collectives: 30.6 us -> none  [body(): left = lax.psum(part_left, 'dp')]
    all_gather x0 -> x1, blocking collectives: none -> 29.1 us  [body(): left = jnp.sum(lax.all_gather(part_left, 'dp'), axis=0)]
    psum x1, blocking collectives: 46.7 us -> 42.8 us  [body(): right, gram = lax.psum((part_right, own_share), ('dp', 'tp'))]
where the time goes in v1:
time: 84.4 us; the launch traced here: 83 us
  blocking collectives  71.9 us (85%)
  other arithmetic  3.99 us (5%)
  matrix products  3.96 us (5%)
  local copies, waits for them, and re-layouts  2.39 us (3%)
    psum x1, blocking collectives, body(): right, gram = lax.psum((part_right, own_share), ('dp', 'tp'))  42.8 us
    all_gather x1, blocking collectives, body(): left = jnp.sum(lax.all_gather(part_left, 'dp'), axis=0)  29.1 us

profile of v1, /device:TPU:14, one launch (start us, length us, event | category | flops | bytes accessed | tf_op | source)
XLA Modules:
  0.0 83.0 jit_solution(18143869499055249514)
XLA Ops:
  0.6 0.0 copy-start
  0.7 0.1 copy.17
  0.8 1.5 %copy-done = bf16[1,2,768,768]{3,2,1,0:T(8,128)(2,1)S(1)} copy-done((bf16[1,2,768,768]{3,2,1,0:T(8,128)(2,1)S(1)}, bf16[1,2,768,768]{3,2,1,0:T(8,128)(2,1)}, u32[]{:S(2)}) %copy-start) | copy-done | bytes 2359320
  2.3 1.5 %fusion.2 = f32[2,768,8]{1,2,0:T(8,128)S(1)} fusion(bf16[1,2,768,768]{3,2,1,0:T(8,128)(2,1)S(1)} %copy-done, f32[2,768,8]{1,2,0:T(8,128)} %param.4), kind=kOutput, calls=%fused_computation.3 | convolution fusion | flops 18886656 | bytes 2457600 | tf_op jit(solution)/shard_map/liw,lwr->lir/dot_general | solution.py:11
  3.8 29.1 %all-gather = f32[16,768,8]{1,2,0:T(8,128)S(1)} all-gather(f32[2,768,8]{1,2,0:T(8,128)S(1)} %fusion.2), channel_id=2, replica_groups=mesh['dp'=8,'tp'=4] {'dp'}, dimensions={0}, use_global_device_ids=true | all-gather | bytes 442368 | tf_op jit(solution)/shard_map/all_gather | solution.py:14
  32.9 0.2 convolution_multiply_fusion.1
  33.1 0.4 fusion.5
  33.6 42.8 %all-reduce = (f32[2,8,8]{1,2,0:T(8,128)S(1)}, f32[2,768,8]{1,2,0:T(8,128)S(1)}) all-reduce(f32[2,8,8]{1,2,0:T(8,128)S(1)} %convolution_multiply_fusion.1, f32[2,768,8]{1,2,0:T(8,128)S(1)} %fusion.5), channel_id=1, replica_groups=mesh['dp'=8,'tp'=4] {'dp','tp'}, use_global_device_ids=true, to_apply=%region_1.0 | all-reduce | flops 12416 | bytes 99328 | tf_op jit(solution)/shard_map/psum | solution.py:21
  76.4 0.1 multiply_reduce_fusion
  76.5 0.1 copy.19
  76.6 0.6 gather_fusion
  77.2 0.1 multiply_add_fusion
  77.3 0.1 copy.20
  77.4 0.1 fusion.14
  77.4 1.4 %custom-call.9 = f32[2,8,8]{2,1,0:T(8,128)S(1)} custom-call(f32[2,8,8]{2,1,0:T(8,128)S(1)} %fusion.14), custom_call_target="Cholesky" | custom-call | tf_op jit(solution)/shard_map/jit(cholesky)/cholesky | solution.py:27
  78.9 0.1 select_reduce_fusion
  78.9 0.1 compare_reduce_fusion
  79.1 0.1 select_bitcast_fusion
  79.1 1.3 %custom-call.10 = f32[2,1,8,8]{2,3,1,0:T(8,128)S(1)} custom-call(f32[2,1,8,8]{3,2,1,0:T(8,128)S(1)} %select_bitcast_fusion), custom_call_target="InvertDiagBlocksLowerTriangular" | custom-call | tf_op jit(solution)/shard_map/triangular_solve | solution.py:31
  80.4 0.2 fusion.10
  80.6 0.1 fusion.12
  80.8 0.7 broadcast_multiply_fusion
  81.5 0.0 copy-done.1
  81.5 1.5 %fusion.4 = f32[2,768,96]{1,2,0:T(8,128)} fusion(f32[2,768,96]{1,2,0:T(8,128)S(1)} %copy-done.1, f32[2,768,8]{1,2,0:T(8,128)S(1)} %reduce_sum.27, f32[2,8,96]{2,1,0:T(8,128)S(1)} %fusion.12), kind=kOutput, calls=%fused_computation.6 | convolution fusion | flops 14450688 | bytes 1234944 | tf_op jit(solution)/shard_map/lir,lrw->liw/dot_general | solution.py:32
  (9 shorter events, 0.1 us)
Async XLA Ops:
  0.6 1.7 %copy-start = (bf16[1,2,768,768]{3,2,1,0:T(8,128)(2,1)S(1)}, bf16[1,2,768,768]{3,2,1,0:T(8,128)(2,1)}, u32[]{:S(2)}) copy-start(bf16[1,2,768,768]{3,2,1,0:T(8,128)(2,1)} %param.3) | copy-start | bytes 7077892
  3.8 77.7 %copy-start.1 = (f32[2,768,96]{1,2,0:T(8,128)S(1)}, f32[2,768,96]{1,2,0:T(8,128)}, u32[]{:S(2)}) copy-start(f32[2,768,96]{1,2,0:T(8,128)} %param.5) | copy-start | bytes 1769476

commit v2 on v0

--- a/solution.py
+++ b/solution.py
@@ -18,7 +18,7 @@
         "liw,lir->lwr", own_grads, small_left, preferred_element_type=jnp.float32
     )
     own_share = part_gram / lax.axis_size("dp")
-    right, gram = lax.psum((part_right, own_share), ("dp", "tp"))
+    right, gram = lax.psum(lax.psum((part_right, own_share), "tp"), "dp")
     gram = gram + 0.001 * jnp.mean(jnp.diagonal(gram, axis1=1, axis2=2), axis=1)[
         :, None, None
     ] * jnp.eye(RANK, dtype=jnp.float32)

time: 88.6 us -> 94.7 us (1.069)
  the two profiles are of different devices: /device:TPU:14 before, /device:TPU:0 now
where the time goes in v2:
time: 94.7 us; the launch traced here: 94.5 us
  blocking collectives  83.4 us (88%)
  matrix products  4.02 us (4%)
  other arithmetic  3.96 us (4%)
  local copies, waits for them, and re-layouts  2.39 us (3%)
    psum x2, blocking collectives, body(): right, gram = lax.psum(lax.psum((part_right, own_share), 'tp'), 'dp')  44.1 us
    psum x1, blocking collectives, body(): left = lax.psum(part_left, 'dp')  39.3 us

profile of v2, /device:TPU:0, one launch (start us, length us, event | category | flops | bytes accessed | tf_op | source)
XLA Modules:
  0.0 94.5 jit_solution(12767856325841215852)
XLA Ops:
  0.6 0.0 copy-start
  0.7 0.1 copy.11
  0.8 1.5 %copy-done = bf16[1,2,768,768]{3,2,1,0:T(8,128)(2,1)S(1)} copy-done((bf16[1,2,768,768]{3,2,1,0:T(8,128)(2,1)S(1)}, bf16[1,2,768,768]{3,2,1,0:T(8,128)(2,1)}, u32[]{:S(2)}) %copy-start) | copy-done | bytes 2359320
  2.3 1.6 %fusion.2 = f32[2,768,8]{1,2,0:T(8,128)S(1)} fusion(bf16[1,2,768,768]{3,2,1,0:T(8,128)(2,1)S(1)} %copy-done, f32[2,768,8]{1,2,0:T(8,128)} %param.4), kind=kOutput, calls=%fused_computation.3 | convolution fusion | flops 18886656 | bytes 2457600 | tf_op jit(solution)/shard_map/liw,lwr->lir/dot_general | solution.py:11
  3.9 39.3 %psum.35 = f32[2,768,8]{1,2,0:T(8,128)S(1)} all-reduce(f32[2,768,8]{1,2,0:T(8,128)S(1)} %fusion.2), channel_id=1, replica_groups=mesh['dp'=8,'tp'=4] {'dp'}, use_global_device_ids=true, to_apply=%region_0.0 | all-reduce | flops 12288 | bytes 98304 | tf_op jit(solution)/shard_map/psum | solution.py:14
  43.2 0.2 convolution_multiply_fusion.1
  43.4 0.4 fusion.5
  43.8 10.7 %all-reduce.1 = (f32[2,8,8]{1,2,0:T(8,128)S(1)}, f32[2,768,8]{1,2,0:T(8,128)S(1)}) all-reduce(f32[2,8,8]{1,2,0:T(8,128)S(1)} %convolution_multiply_fusion.1, f32[2,768,8]{1,2,0:T(8,128)S(1)} %fusion.5), channel_id=1, replica_groups=mesh['dp'=8,'tp'=4] {'tp'}, use_global_device_ids=true, to_apply=%region_1.0 | all-reduce | flops 12416 | bytes 99328 | tf_op jit(solution)/shard_map/psum | solution.py:21
  54.5 33.4 %all-reduce = (f32[2,8,8]{1,2,0:T(8,128)S(1)}, f32[2,768,8]{1,2,0:T(8,128)S(1)}) all-reduce(f32[2,8,8]{1,2,0:T(8,128)S(1)} %get-tuple-element.4, f32[2,768,8]{1,2,0:T(8,128)S(1)} %get-tuple-element.5), channel_id=1, replica_groups=mesh['dp'=8,'tp'=4] {'dp'}, use_global_device_ids=true, to_apply=%region_2.0 | all-reduce | flops 12416 | bytes 99328 | tf_op jit(solution)/shard_map/psum | solution.py:21
  87.9 0.1 multiply_reduce_fusion
  88.0 0.1 copy.13
  88.1 0.6 gather_fusion
  88.7 0.1 multiply_add_fusion
  88.8 0.1 copy.14
  88.9 0.1 fusion.14
  89.0 1.4 %custom-call.9 = f32[2,8,8]{2,1,0:T(8,128)S(1)} custom-call(f32[2,8,8]{2,1,0:T(8,128)S(1)} %fusion.14), custom_call_target="Cholesky" | custom-call | tf_op jit(solution)/shard_map/jit(cholesky)/cholesky | solution.py:27
  90.4 0.1 select_reduce_fusion
  90.5 0.1 compare_reduce_fusion
  90.6 0.1 select_bitcast_fusion
  90.7 1.3 %custom-call.10 = f32[2,1,8,8]{2,3,1,0:T(8,128)S(1)} custom-call(f32[2,1,8,8]{3,2,1,0:T(8,128)S(1)} %select_bitcast_fusion), custom_call_target="InvertDiagBlocksLowerTriangular" | custom-call | tf_op jit(solution)/shard_map/triangular_solve | solution.py:31
  91.9 0.2 fusion.10
  92.2 0.1 fusion.12
  92.3 0.7 broadcast_multiply_fusion
  93.0 1.5 %fusion.4 = f32[2,768,96]{1,2,0:T(8,128)} fusion(f32[2,768,96]{1,2,0:T(8,128)S(1)} %copy-done.1, f32[2,768,8]{1,2,0:T(8,128)S(1)} %psum.35, f32[2,8,96]{2,1,0:T(8,128)S(1)} %fusion.12), kind=kOutput, calls=%fused_computation.6 | convolution fusion | flops 14450688 | bytes 1234944 | tf_op jit(solution)/shard_map/lir,lrw->liw/dot_general | solution.py:32
  (9 shorter events, 0.1 us)
Async XLA Ops:
  0.6 1.7 %copy-start = (bf16[1,2,768,768]{3,2,1,0:T(8,128)(2,1)S(1)}, bf16[1,2,768,768]{3,2,1,0:T(8,128)(2,1)}, u32[]{:S(2)}) copy-start(bf16[1,2,768,768]{3,2,1,0:T(8,128)(2,1)} %param.3) | copy-start | bytes 7077892
  2.3 90.7 %copy-start.1 = (f32[2,768,96]{1,2,0:T(8,128)S(1)}, f32[2,768,96]{1,2,0:T(8,128)}, u32[]{:S(2)}) copy-start(f32[2,768,96]{1,2,0:T(8,128)} %param.5) | copy-start | bytes 1769476
